TPU v7x, 512 devices: a whole 4x8x8 slice. The times are simulated.
512 devices in a mesh: gx: 16 (over y_lo, x, core), gy: 32 (over y_hi, z).
Axes of the slice: x: 4, y: 8 (y_hi: 4, y_lo: 2; y = y_hi * 2 + y_lo), z: 8, core: 2. Of those that a mesh axis runs over, the one named last changes fastest.
Arguments:
- activation: bfloat16 [32, 64, 128, 128], P(None, 'gx', 'gy'), may hold values from -6 to 6
- out_grad: bfloat16 [32, 64, 128, 128], P(None, 'gx', 'gy'), may hold values from -6 to 6
- kernel: bfloat16 [3, 3, 3, 32, 32], replicated, may hold values from -0.21875 to 0.21875
Outputs:
- grad_input: bfloat16 [32, 64, 128, 128], P(None, 'gx', 'gy')
- grad_kernel: float32 [3, 3, 3, 32, 32], replicated
All inputs are finite; a program needn't handle non-finite values.
Results may differ from a plain program's by a relative error of at most 0.001.
Values may be sent and summed in bfloat16 or wider, within the bound.
A program may use at most 64 MiB of HBM per device.

v0:
```python
import jax
import jax.numpy as jnp
from jax import lax
from jax.sharding import PartitionSpec as P


def extended(cells, sides, width):
    for axis, dim in sides:
        count = lax.axis_size(axis)
        ends = count - 1
        head = lax.slice_in_dim(cells, 0, width, axis=dim)
        tail = lax.slice_in_dim(cells, cells.shape[dim] - width, cells.shape[dim], axis=dim)
        cells = jnp.concatenate(
            [
                lax.ppermute(tail, axis, [(i, (i + 1) % count) for i in range(ends)]),
                cells,
                lax.ppermute(head, axis, [((i + 1) % count, i) for i in range(ends)]),
            ],
            axis=dim,
        )
    return cells


def padded_z(block):
    return jnp.pad(block, ((0, 0), (0, 0), (0, 0), (1, 1)))


def contract_cells(left, right):
    return lax.dot_general(
        left, right, (((1,), (1,)), ((), ())), preferred_element_type=jnp.float32
    )


def shards(activation, out_grad, kernel):
    channels = activation.shape[0]
    size_x, size_y, size_z = (activation.shape[1], activation.shape[2], activation.shape[3])
    cell_count = size_x * size_y * size_z
    grad_pad = padded_z(extended(out_grad, (("gx", 1), ("gy", 2)), 1))
    flat_act = activation.reshape(channels, cell_count)
    accumulated = jnp.zeros((channels, cell_count), jnp.float32)
    products = []
    for off_x in range(3):
        for off_y in range(3):
            for off_z in range(3):
                window = grad_pad[
                    :,
                    2 - off_x : 2 - off_x + size_x,
                    2 - off_y : 2 - off_y + size_y,
                    2 - off_z : 2 - off_z + size_z,
                ].reshape(channels, cell_count)
                accumulated = accumulated + jnp.dot(
                    kernel[off_x, off_y, off_z].T, window, preferred_element_type=jnp.float32
                )
                products.append(contract_cells(window, flat_act))
    grad_input = accumulated.reshape(channels, size_x, size_y, size_z).astype(jnp.bfloat16)
    local_terms = jnp.stack(products).reshape(3, 3, 3, channels, channels)
    summed = lax.psum(local_terms, ("gx", "gy"))
    total_cells = size_x * lax.axis_size("gx") * size_y * lax.axis_size("gy") * size_z
    grad_kernel = summed / jnp.sqrt(jnp.float32(total_cells))
    return (grad_input, grad_kernel)


def solution(mesh):
    return jax.shard_map(
        shards,
        mesh=mesh,
        in_specs=(P(None, "gx", "gy", None), P(None, "gx", "gy", None), P()),
        out_specs=(P(None, "gx", "gy", None), P()),
        check_vma=False,
    )
```

profile of v0, /device:TPU:1, one launch (start us, length us, event | category | flops | bytes accessed | tf_op | source)
XLA Modules:
  0.0 321.6 jit_solution(15597050109210917057)
XLA Ops:
  8.1 4.5 %collective-permute-start = (bf16[32,1,4,128]{3,0,2,1:T(8,128)(2,1)S(1)}, bf16[32,1,4,128]{3,0,2,1:T(8,128)(2,1)S(1)}, u32[]{:S(2)}, u32[]{:S(2)}) collective-permute-start(bf16[32,1,4,128]{3,0,2,1:T(8,128)(2,1)S(1)} %copy.183), channel_id=1, source_target_pairs={{0,32},{32,64},{64,96},{96,128},{128,160},{160,192},{192,224},{224... | collective-permute-start | bytes 98312 | tf_op jit(solution)/shard_map/ppermute | solution.py:15
  12.6 5.5 %collective-permute-start.1 = (bf16[32,1,4,128]{3,0,2,1:T(8,128)(2,1)S(1)}, bf16[32,1,4,128]{3,0,2,1:T(8,128)(2,1)S(1)}, u32[]{:S(2)}, u32[]{:S(2)}) collective-permute-start(bf16[32,1,4,128]{3,0,2,1:T(8,128)(2,1)S(1)} %copy.184), channel_id=1, source_target_pairs={{32,0},{64,32},{96,64},{128,96},{160,128},{192,160},{224,192},{256... | collective-permute-start | bytes 98312 | tf_op jit(solution)/shard_map/ppermute | solution.py:17
  18.2 1.6 reshape.104
  20.0 1.9 collective-permute-start.2
  21.9 1.3 collective-permute-start.3
  25.1 2.3 collective-permute-done.3
  27.7 1.3 fusion.161
  57.0 1.1 convolution_bitcast_fusion.10
  58.9 1.0 reshape.110
  60.8 1.2 convolution_add_fusion.12
  62.0 1.0 convolution_add_fusion.11
  63.0 1.0 convolution_add_fusion.10
  64.0 1.0 convolution_add_fusion.9
  65.0 1.0 convolution_add_fusion.8
  66.0 1.0 convolution_add_fusion.7
  66.9 1.0 convolution_add_fusion.6
  67.9 1.0 convolution_add_fusion.5
  68.9 1.0 convolution_add_fusion.4
  69.9 1.0 convolution_add_fusion.3
  70.9 1.0 convolution_add_fusion.2
  71.9 1.0 fusion.13
  73.8 1.0 fusion.14
  75.5 237.4 %all-reduce.3.cloned.1.call-done = f32[3,3,3,32,32]{4,3,2,1,0:T(8,128)} async-done(((f32[3,3,3,32,32]{4,3,2,1,0:T(8,128)}), f32[3,3,3,32,32]{4,3,2,1,0:T(8,128)}) %all-reduce.3.cloned.1.call-update) | async-done | bytes 110608 | tf_op jit(solution)/shard_map/psum | solution.py:57
  312.9 1.8 broadcast_multiply_fusion
  (150 shorter events, 34.4 us)
Async XLA Ops:
  7.2 21.7 %copy-start = (bf16[32,4,4,128]{3,2,1,0:T(4,128)(2,1)S(1)}, bf16[32,4,4,128]{3,2,1,0:T(4,128)(2,1)}, u32[]{:S(2)}) copy-start(bf16[32,4,4,128]{3,2,1,0:T(4,128)(2,1)} %param.3) | copy-start | bytes 393220
  7.2 12.6 %copy-start.1 = (bf16[32,4,4,128]{3,2,1,0:T(4,128)(2,1)S(1)}, bf16[32,4,4,128]{3,2,1,0:T(4,128)(2,1)}, u32[]{:S(2)}) copy-start(bf16[32,4,4,128]{3,2,1,0:T(4,128)(2,1)} %param.4) | copy-start | bytes 393220
  7.2 305.8 %all-reduce.3.cloned.1.call-start = ((), (), s32[]{:S(2)}) async-start(), calls=%async_computation | async-start | bytes 884736 | tf_op jit(solution)/shard_map/psum | solution.py:57
  8.1 11.7 %collective-permute-start = (bf16[32,1,4,128]{3,0,2,1:T(8,128)(2,1)S(1)}, bf16[32,1,4,128]{3,0,2,1:T(8,128)(2,1)S(1)}, u32[]{:S(2)}, u32[]{:S(2)}) collective-permute-start(bf16[32,1,4,128]{3,0,2,1:T(8,128)(2,1)S(1)} %copy.183), channel_id=1, source_target_pairs={{0,32},{32,64},{64,96},{96,128},{128,160},{160,192},{192,224},{224... | collective-permute-start | bytes 98312 | tf_op jit(solution)/shard_map/ppermute | solution.py:15
  12.6 7.3 %collective-permute-start.1 = (bf16[32,1,4,128]{3,0,2,1:T(8,128)(2,1)S(1)}, bf16[32,1,4,128]{3,0,2,1:T(8,128)(2,1)S(1)}, u32[]{:S(2)}, u32[]{:S(2)}) collective-permute-start(bf16[32,1,4,128]{3,0,2,1:T(8,128)(2,1)S(1)} %copy.184), channel_id=1, source_target_pairs={{32,0},{64,32},{96,64},{128,96},{160,128},{192,160},{224,192},{256... | collective-permute-start | bytes 98312 | tf_op jit(solution)/shard_map/ppermute | solution.py:17
  20.0 5.1 %collective-permute-start.2 = (bf16[32,6,1,128]{3,0,2,1:T(8,128)(2,1)S(1)}, bf16[32,6,1,128]{3,0,2,1:T(8,128)(2,1)S(1)}, u32[]{:S(2)}, u32[]{:S(2)}) collective-permute-start(bf16[32,6,1,128]{3,0,2,1:T(8,128)(2,1)S(1)} %get-tuple-element.29), channel_id=1, source_target_pairs={{0,1},{1,2},{2,3},{3,4},{4,5},{5,6},{6,7},{7,8},{8,9},{9,10},{10,1... | collective-permute-start | bytes 147464 | tf_op jit(solution)/shard_map/ppermute | solution.py:15
  21.9 5.5 %collective-permute-start.3 = (bf16[32,6,1,128]{3,0,2,1:T(8,128)(2,1)S(1)}, bf16[32,6,1,128]{3,0,2,1:T(8,128)(2,1)S(1)}, u32[]{:S(2)}, u32[]{:S(2)}) collective-permute-start(bf16[32,6,1,128]{3,0,2,1:T(8,128)(2,1)S(1)} %get-tuple-element.30), channel_id=1, source_target_pairs={{1,0},{2,1},{3,2},{4,3},{5,4},{6,5},{7,6},{8,7},{9,8},{10,9},{11,1... | collective-permute-start | bytes 147464 | tf_op jit(solution)/shard_map/ppermute | solution.py:17
  36.8 1.6 copy-start.3
  39.2 1.6 copy-start.7
  53.3 1.8 copy-start.4
  54.4 1.8 copy-start.2
  59.8 2.2 copy-start.11
  60.8 2.2 copy-start.13
  62.0 2.0 copy-start.9
  63.0 2.0 copy-start.10
  64.0 2.0 copy-start.12
  65.0 2.0 copy-start.14
  65.9 2.0 copy-start.15
  66.9 2.0 copy-start.16
  67.9 2.0 copy-start.17
  68.9 2.0 copy-start.18
  69.9 2.0 copy-start.19
  70.9 2.0 copy-start.8
  71.9 1.9 copy-start.6
  (2 other events, 2.4 us)
Sparse Core Ops, SparseCore 0:
  35.1 277.8 all-reduce.2
where the time goes:
time: 323 us; the launch traced here: 322 us
  waiting for transfers between devices  240 us (74%)
  matrix products  31 us (10%)
  local copies, waits for them, and re-layouts  19.9 us (6%)
  between operations  14.8 us (5%)
  starting transfers between devices  13.3 us (4%)
    psum x1, waiting for transfers between devices, shards(): summed = lax.psum(local_terms, ('gx', 'gy'))  237 us
    dot_general x27, matrix products, shards(): jnp.dot(kernel[off_x, off_y, off_z].T, window, preferred_element_type=jnp...  25.8 us
    reshape x27, local copies, waits for them, and re-layouts, shards(): window = grad_pad[:, 2 - off_x:2 - off_x + size_x, 2 - off_y:2 - off_y +...  13.6 us
    ppermute x2, starting transfers between devices, extended(): lax.ppermute(head, axis, [((i + 1) % count, i) for i in range(ends)])  6.83 us
  transfers between devices with their start and end apart: 5, of which 2 were waited for; matrix products, arithmetic and copies ran while one was open for 14% of the time, Pallas kernels for 0%

commit v1 on v0

v1 whole, which is shorter than its diff:
```python
import functools
import math

import jax
import jax.numpy as jnp
from jax import lax
from jax.experimental import pallas as pl
from jax.experimental.pallas import tpu as pltpu
from jax.sharding import PartitionSpec as P

MESH = pl.DeviceIdType.MESH
F32 = jnp.float32
BF16 = jnp.bfloat16
LOW = 2


def far_first(count):
    return sorted(range(1, count), key=lambda d: -min(d, count - d))


def kernel(
    sizes, scale, act_ref, g_ref, k_ref, gi_ref, gk_ref,
    rows, halo, acts, total, kmat, part, from_a, sum_a, from_y, from_z, final,
    halo_send, halo_recv, a_send, a_recv, y_send, y_recv, z_send, z_recv,
    yg_send, yg_recv, ag_send, ag_recv,
):
    n_gx, n_gy, n_a, n_y, n_z, chans, size_x, size_y, size_z = sizes
    cols = size_x * size_y
    gx = lax.axis_index("gx")
    gy = lax.axis_index("gy")
    a = lax.rem(gx, n_a)
    y = lax.div(gy, n_z) * LOW + lax.div(gx, n_a)
    z = lax.rem(gy, n_z)

    def a_peer(d):
        return (lax.div(gx, n_a) * n_a + lax.rem(a + d, n_a), gy)

    def y_peer(d):
        other = lax.rem(y + d, n_y)
        return (lax.rem(other, LOW) * n_a + a, lax.div(other, LOW) * n_z + z)

    def z_peer(d):
        return (gx, lax.div(gy, n_z) * n_z + lax.rem(z + d, n_z))

    def halo_peer(dx, dy):
        return (lax.rem(gx + dx + n_gx, n_gx), lax.rem(gy + dy + n_gy, n_gy))

    steps = [(dx, dy) for dx in (-1, 0, 1) for dy in (-1, 0, 1) if dx or dy]
    steps.sort(key=lambda s: -abs(s[0]) - 2 * abs(s[1]))
    peers = [halo_peer(*s) for s in steps]
    peers += [a_peer(d) for d in far_first(n_a)]
    peers += [y_peer(d) for d in far_first(n_y)]
    peers += [z_peer(d) for d in far_first(n_z)]
    barrier = pltpu.get_barrier_semaphore()
    for peer in peers:
        pl.semaphore_signal(barrier, inc=1, device_id=peer, device_id_type=MESH)

    rows[...] = g_ref[...].astype(F32)
    for i in range(size_x):
        for j in range(size_y):
            col = rows[pl.ds(i * size_y + j, chans, stride=cols), :]
            halo[i + 1, j + 1] = col.astype(BF16)

    pl.semaphore_wait(barrier, len(peers))

    def span(step, size):
        if step == 0:
            return slice(1, size + 1), slice(1, size + 1)
        return (slice(size, size + 1), slice(0, 1)) if step > 0 else (slice(1, 2), slice(size + 1, size + 2))

    copies = []
    for n, (dx, dy) in enumerate(steps):
        src_x, dst_x = span(dx, size_x)
        src_y, dst_y = span(dy, size_y)
        copy = pltpu.make_async_remote_copy(
            src_ref=halo.at[src_x, src_y],
            dst_ref=halo.at[dst_x, dst_y],
            send_sem=halo_send.at[n],
            recv_sem=halo_recv.at[n],
            device_id=halo_peer(dx, dy),
            device_id_type=MESH,
        )
        copy.start()
        copies.append(copy)

    lane = lax.broadcasted_iota(jnp.int32, (chans, size_z), 1)

    def shifted(tile, step):
        if step == 0:
            return tile
        moved = pltpu.roll(tile, step % size_z, 1)
        edge = 0 if step > 0 else size_z - 1
        return jnp.where(lane == edge, 0.0, moved)

    rows[...] = act_ref[...].astype(F32)
    for i in range(size_x):
        for j in range(size_y):
            col = rows[pl.ds(i * size_y + j, chans, stride=cols), :]
            for c in range(3):
                acts[i, j, pl.ds(c * chans, chans)] = shifted(col, 1 - c).astype(BF16)

    for copy in copies:
        copy.wait_recv()

    def blank(index):
        halo[index] = jnp.zeros(halo.at[index].shape, BF16)

    @pl.when(gx == 0)
    def _():
        blank((slice(0, 1),))

    @pl.when(gx == n_gx - 1)
    def _():
        blank((slice(size_x + 1, size_x + 2),))

    @pl.when(gy == 0)
    def _():
        blank((slice(None), slice(0, 1)))

    @pl.when(gy == n_gy - 1)
    def _():
        blank((slice(None), slice(size_y + 1, size_y + 2)))

    def windows(i):
        columns = []
        for j in range(size_y):
            tiles = [halo[i + 2 - off_x, j + 2 - off_y] for off_x in range(3) for off_y in range(3)]
            columns.append(jnp.concatenate(tiles, axis=0))
        return jnp.concatenate(columns, axis=1)

    total[...] = jnp.zeros_like(total)
    for i in range(size_x):
        right = jnp.concatenate([acts[i, j] for j in range(size_y)], axis=1)
        total[:, 0 : 3 * chans] += lax.dot_general(
            windows(i), right, (((1,), (1,)), ((), ())), preferred_element_type=F32
        )

    piece = part.shape[2]

    def put(row, block):
        for s in range(0, chans, piece):
            at = (row * chans + s) // piece
            part[at // n_y, at % n_y] = block[s : s + piece]

    wide = lax.broadcasted_iota(jnp.int32, (chans, 4 * chans), 1)
    for r in range(8):
        if r == 7:
            put(r, jnp.zeros((chans, 4 * chans), F32))
            continue
        block = total[pl.ds(r * chans, chans), :]
        if r < 6:
            extra = total[pl.ds((7 + r // 3) * chans, chans), :]
            extra = pltpu.roll(extra, (3 - r % 3) * chans, 1)
            block = jnp.where(wide < 3 * chans, block, extra)
        put(r, block)

    def send(src, dst, send_sem, recv_sem, peer):
        copy = pltpu.make_async_remote_copy(
            src_ref=src, dst_ref=dst, send_sem=send_sem, recv_sem=recv_sem,
            device_id=peer, device_id_type=MESH,
        )
        copy.start()
        copies.append(copy)
        return copy

    flying = [
        send(part.at[lax.rem(a + d, n_a)], from_a.at[d], a_send.at[d], a_recv.at[d], a_peer(d))
        for d in far_first(n_a)
    ]

    kmat[...] = jnp.zeros_like(kmat)
    for ab in range(9):
        for c in range(3):
            kmat[pl.ds(ab * chans, chans), pl.ds(c * chans, chans)] = k_ref[
                pl.ds((ab * 3 + c) * chans, chans), :
            ].astype(F32)
    left = kmat[...].T[0 : 3 * chans, 0 : 9 * chans].astype(BF16)
    for i in range(size_x):
        sums = jnp.dot(left, windows(i), preferred_element_type=F32)
        for j in range(size_y):
            tile = sums[:, j * size_z : (j + 1) * size_z]
            value = shifted(tile[0:chans], -1) + tile[chans : 2 * chans] + shifted(tile[2 * chans :], 1)
            rows[pl.ds(i * size_y + j, chans, stride=cols), :] = value
    gi_ref[...] = rows[...].astype(BF16)

    def arrived(flying):
        for copy in flying:
            copy.wait_recv()

    arrived(flying)
    value = part[a]
    for d in range(1, n_a):
        value = value + from_a[d]
    sum_a[...] = value
    flying = [
        send(sum_a.at[lax.rem(y + d, n_y)], from_y.at[d], y_send.at[d], y_recv.at[d], y_peer(d))
        for d in far_first(n_y)
    ]
    arrived(flying)
    value = sum_a[y]
    for d in range(1, n_y):
        value = value + from_y[d]
    from_z[z] = value
    flying = [
        send(from_z.at[z], from_z.at[z], z_send.at[d], z_recv.at[d], z_peer(d))
        for d in far_first(n_z)
    ]
    arrived(flying)
    value = from_z[0]
    for d in range(1, n_z):
        value = value + from_z[d]
    final[a, y] = value * scale
    flying = [
        send(final.at[a, y], final.at[a, y], yg_send.at[d], yg_recv.at[d], y_peer(d))
        for d in far_first(n_y)
    ]
    arrived(flying)
    flying = [
        send(final.at[a], final.at[a], ag_send.at[d], ag_recv.at[d], a_peer(d))
        for d in far_first(n_a)
    ]
    arrived(flying)

    for r in range(7):
        for s in range(0, chans, piece):
            at = (r * chans + s) // piece
            block = final[at // n_y, at % n_y]
            for c in range(4):
                if c < 3:
                    place = r * 3 + c
                elif r < 6:
                    place = 21 + r
                else:
                    continue
                gk_ref[pl.ds(place * chans + s, piece), :] = block[:, c * chans : (c + 1) * chans]

    for copy in copies:
        copy.wait_send()


def solution(mesh):
    n_gx, n_gy = mesh.shape["gx"], mesh.shape["gy"]
    n_a = n_gx // LOW
    n_z = 8 if n_gy % 8 == 0 else 2
    n_y = n_gy // n_z * LOW

    def step(activation, out_grad, weights):
        chans, size_x, size_y, size_z = activation.shape
        cols = size_x * size_y
        cells = n_gx * size_x * n_gy * size_y * size_z
        piece = 8 * chans // (n_a * n_y)
        sizes = (n_gx, n_gy, n_a, n_y, n_z, chans, size_x, size_y, size_z)
        vmem = pl.BlockSpec(memory_space=pltpu.VMEM)
        dma = pltpu.SemaphoreType.DMA
        grad_input, grad_kernel = pl.pallas_call(
            functools.partial(kernel, sizes, 1.0 / math.sqrt(cells)),
            out_shape=(
                jax.ShapeDtypeStruct((chans * cols, size_z), BF16),
                jax.ShapeDtypeStruct((27 * chans, chans), F32),
            ),
            in_specs=[vmem] * 3,
            out_specs=(vmem, vmem),
            scratch_shapes=[
                pltpu.VMEM((chans * cols, size_z), F32),
                pltpu.VMEM((size_x + 2, size_y + 2, chans, size_z), BF16),
                pltpu.VMEM((size_x, size_y, 3 * chans, size_z), BF16),
                pltpu.VMEM((9 * chans, 4 * chans), F32),
                pltpu.VMEM((12 * chans, 4 * chans), F32),
                pltpu.VMEM((n_a, n_y, piece, 4 * chans), F32),
                pltpu.VMEM((n_a, n_y, piece, 4 * chans), F32),
                pltpu.VMEM((n_y, piece, 4 * chans), F32),
                pltpu.VMEM((n_y, piece, 4 * chans), F32),
                pltpu.VMEM((n_z, piece, 4 * chans), F32),
                pltpu.VMEM((n_a, n_y, piece, 4 * chans), F32),
                dma((8,)), dma((8,)),
                dma((n_a,)), dma((n_a,)),
                dma((n_y,)), dma((n_y,)),
                dma((n_z,)), dma((n_z,)),
                dma((n_y,)), dma((n_y,)),
                dma((n_a,)), dma((n_a,)),
            ],
            compiler_params=pltpu.CompilerParams(collective_id=0, has_side_effects=True),
        )(
            activation.reshape(chans * cols, size_z),
            out_grad.reshape(chans * cols, size_z),
            weights.reshape(27 * chans, chans),
        )
        return (
            grad_input.reshape(chans, size_x, size_y, size_z),
            grad_kernel.reshape(3, 3, 3, chans, chans),
        )

    return jax.shard_map(
        step,
        mesh=mesh,
        in_specs=(P(None, "gx", "gy", None), P(None, "gx", "gy", None), P()),
        out_specs=(P(None, "gx", "gy", None), P()),
        check_vma=False,
    )
```

time: 323 us -> 48.3 us (0.15)
  waiting for transfers between devices: 240 us -> 0 us
  Pallas kernels: 0 us -> 44.1 us
  matrix products: 31 us -> 0 us
  local copies, waits for them, and re-layouts: 19.9 us -> 3.41 us
  between operations: 14.8 us -> 0.64 us
  starting transfers between devices: 13.3 us -> 0 us
    psum x1 -> x0, waiting for transfers between devices: 237 us -> none  [shards(): summed = lax.psum(local_terms, ('gx', 'gy'))]
    pallas_call x0 -> x1, Pallas kernels: none -> 44.1 us  [step(): pl.pallas_call(functools.partial(kernel, sizes, 1.0 / math.sqrt(cells)),...]
    dot_general x54 -> x0, matrix products: 31 us -> none  [the longest x27 25.8 us: shards(): jnp.dot(kernel[off_x, off_y, off_z].T, window, preferred_element_type=jnp...]
    reshape x27 -> x0, local copies, waits for them, and re-layouts: 13.6 us -> none  [shards(): window = grad_pad[:, 2 - off_x:2 - off_x + size_x, 2 - off_y:2 - off_y +...]
    ppermute x4 -> x0, starting transfers between devices: 13.2 us -> none  [the longest x2 6.83 us: extended(): lax.ppermute(head, axis, [((i + 1) % count, i) for i in range(ends)])]
    slice x31 -> x0, local copies, waits for them, and re-layouts: 4.57 us -> none  [the longest x29 3.73 us: shards(): grad_pad[:, 2 - off_x:2 - off_x + size_x, 2 - off_y:2 - off_y + size_y, 2...]
  transfers between devices with their start and end apart: 5 -> 0, of which waited for: 2 -> 0; matrix products, arithmetic and copies ran while one was open for 14% -> 0% of each run, Pallas kernels for 0% -> 0%
where the time goes in v1:
time: 48.3 us; the launch traced here: 48.1 us
  Pallas kernels  44.1 us (91%)
  local copies, waits for them, and re-layouts  3.41 us (7%)
  between operations  0.64 us (1%)
    pallas_call x1, Pallas kernels, step(): pl.pallas_call(functools.partial(kernel, sizes, 1.0 / math.sqrt(cells)),...  44.1 us
    unnamed x2, local copies, waits for them, and re-layouts  3.41 us

profile of v1, /device:TPU:1, one launch (start us, length us, event | category | flops | bytes accessed | tf_op | source)
XLA Modules:
  0.0 48.1 jit_solution(1202074051579366020)
XLA Ops:
  0.6 44.1 %shard_map.50 = (bf16[512,128]{1,0:T(8,128)(2,1)}, f32[864,32]{1,0:T(8,128)}) custom-call(bf16[512,128]{1,0:T(8,128)(2,1)} %bitcast.8, bf16[512,128]{1,0:T(8,128)(2,1)} %bitcast.9, bf16[864,32]{1,0:T(8,128)(2,1)} %bitcast.6), custom_call_target="tpu_custom_call" | custom-call | tf_op jit(solution)/shard_map/pallas_call | solution.py:255
  44.7 1.6 %copy.7 = bf16[32,4,4,128]{3,2,1,0:T(4,128)(2,1)} copy(bf16[32,4,4,128]{3,2,1,0:T(4,128)(2,1)} %bitcast.7) | data formatting | bytes 262144
  46.3 1.8 %copy.8 = f32[3,3,3,32,32]{4,3,2,1,0:T(8,128)} copy(f32[3,3,3,32,32]{4,3,2,1,0:T(8,128)} %bitcast.5) | data formatting | bytes 221184

commit v2 on v1

--- a/solution.py
+++ b/solution.py
@@ -19,8 +19,8 @@
 
 
 def kernel(
-    sizes, scale, act_ref, g_ref, k_ref, gi_ref, gk_ref,
-    rows, halo, acts, total, kmat, part, from_a, sum_a, from_y, from_z, final,
+    sizes, scale, act_hbm, g_hbm, k_hbm, gi_ref, gk_ref,
+    act_ref, g_ref, k_ref, loaded, rows, halo, acts, total, kmat, part, from_a, sum_a, from_y, from_z, final,
     halo_send, halo_recv, a_send, a_recv, y_send, y_recv, z_send, z_recv,
     yg_send, yg_recv, ag_send, ag_recv,
 ):
@@ -55,6 +55,14 @@
     for peer in peers:
         pl.semaphore_signal(barrier, inc=1, device_id=peer, device_id_type=MESH)
 
+    loads = [
+        pltpu.make_async_copy(src, dst, loaded.at[n])
+        for n, (src, dst) in enumerate([(g_hbm, g_ref), (act_hbm, act_ref), (k_hbm, k_ref)])
+    ]
+    for load in loads:
+        load.start()
+
+    loads[0].wait()
     rows[...] = g_ref[...].astype(F32)
     for i in range(size_x):
         for j in range(size_y):
@@ -92,6 +100,7 @@
         edge = 0 if step > 0 else size_z - 1
         return jnp.where(lane == edge, 0.0, moved)
 
+    loads[1].wait()
     rows[...] = act_ref[...].astype(F32)
     for i in range(size_x):
         for j in range(size_y):
@@ -160,14 +169,18 @@
             device_id=peer, device_id_type=MESH,
         )
         copy.start()
-        copies.append(copy)
-        return copy
-
-    flying = [
-        send(part.at[lax.rem(a + d, n_a)], from_a.at[d], a_send.at[d], a_recv.at[d], a_peer(d))
-        for d in far_first(n_a)
-    ]
-
+
+    def landed(ref, sem):
+        pltpu.make_async_copy(ref, ref, sem).wait()
+
+    for dy in far_first(n_y) + [0]:
+        for d in far_first(n_a):
+            send(
+                part.at[lax.rem(a + d, n_a), lax.rem(y + dy, n_y)], from_a.at[dy, d],
+                a_send, a_recv.at[dy], a_peer(d),
+            )
+
+    loads[2].wait()
     kmat[...] = jnp.zeros_like(kmat)
     for ab in range(9):
         for c in range(3):
@@ -183,43 +196,37 @@
             rows[pl.ds(i * size_y + j, chans, stride=cols), :] = value
     gi_ref[...] = rows[...].astype(BF16)
 
-    def arrived(flying):
-        for copy in flying:
-            copy.wait_recv()
-
-    arrived(flying)
-    value = part[a]
-    for d in range(1, n_a):
-        value = value + from_a[d]
-    sum_a[...] = value
-    flying = [
-        send(sum_a.at[lax.rem(y + d, n_y)], from_y.at[d], y_send.at[d], y_recv.at[d], y_peer(d))
-        for d in far_first(n_y)
-    ]
-    arrived(flying)
-    value = sum_a[y]
+    for dy in far_first(n_y) + [0]:
+        landed(from_a.at[dy, 1:], a_recv.at[dy])
+        value = part[a, lax.rem(y + dy, n_y)]
+        for d in range(1, n_a):
+            value = value + from_a[dy, d]
+        if dy:
+            sum_a[dy] = value
+            send(sum_a.at[dy], from_y.at[dy], y_send, y_recv, y_peer(dy))
+    landed(from_y.at[1:], y_recv)
     for d in range(1, n_y):
         value = value + from_y[d]
+
     from_z[z] = value
-    flying = [
-        send(from_z.at[z], from_z.at[z], z_send.at[d], z_recv.at[d], z_peer(d))
-        for d in far_first(n_z)
-    ]
-    arrived(flying)
+    for d in far_first(n_z):
+        send(from_z.at[z], from_z.at[z], z_send, z_recv, z_peer(d))
+    landed(from_z.at[1:], z_recv)
     value = from_z[0]
     for d in range(1, n_z):
         value = value + from_z[d]
+
     final[a, y] = value * scale
-    flying = [
-        send(final.at[a, y], final.at[a, y], yg_send.at[d], yg_recv.at[d], y_peer(d))
-        for d in far_first(n_y)
-    ]
-    arrived(flying)
-    flying = [
-        send(final.at[a], final.at[a], ag_send.at[d], ag_recv.at[d], a_peer(d))
-        for d in far_first(n_a)
-    ]
-    arrived(flying)
+    for dy in far_first(n_y):
+        send(final.at[a, y], final.at[a, y], yg_send, yg_recv.at[dy], y_peer(dy))
+    for dy in [0] + far_first(n_y)[::-1]:
+        source = lax.rem(y - dy + n_y, n_y)
+        piece_ref = final.at[a, source]
+        if dy:
+            landed(piece_ref, yg_recv.at[dy])
+        for d in far_first(n_a):
+            send(piece_ref, piece_ref, ag_send, ag_recv, a_peer(d))
+    landed(final.at[1:], ag_recv)
 
     for r in range(7):
         for s in range(0, chans, piece):
@@ -236,6 +243,11 @@
 
     for copy in copies:
         copy.wait_send()
+    landed(part.at[1:], a_send)
+    landed(sum_a.at[1:], y_send)
+    landed(from_z.at[1:], z_send)
+    landed(sum_a.at[1:], yg_send)
+    landed(final.at[1:], ag_send)
 
 
 def solution(mesh):
@@ -255,29 +267,33 @@
         grad_input, grad_kernel = pl.pallas_call(
             functools.partial(kernel, sizes, 1.0 / math.sqrt(cells)),
             out_shape=(
-                jax.ShapeDtypeStruct((chans * cols, size_z), BF16),
-                jax.ShapeDtypeStruct((27 * chans, chans), F32),
+                pltpu.VMEM((chans * cols, size_z), BF16),
+                pltpu.VMEM((27 * chans, chans), F32),
             ),
-            in_specs=[vmem] * 3,
+            in_specs=[pl.BlockSpec(memory_space=pl.ANY)] * 3,
             out_specs=(vmem, vmem),
             scratch_shapes=[
+                pltpu.VMEM((chans * cols, size_z), BF16),
+                pltpu.VMEM((chans * cols, size_z), BF16),
+                pltpu.VMEM((27 * chans, chans), BF16),
+                dma((3,)),
                 pltpu.VMEM((chans * cols, size_z), F32),
                 pltpu.VMEM((size_x + 2, size_y + 2, chans, size_z), BF16),
                 pltpu.VMEM((size_x, size_y, 3 * chans, size_z), BF16),
                 pltpu.VMEM((9 * chans, 4 * chans), F32),
                 pltpu.VMEM((12 * chans, 4 * chans), F32),
                 pltpu.VMEM((n_a, n_y, piece, 4 * chans), F32),
-                pltpu.VMEM((n_a, n_y, piece, 4 * chans), F32),
+                pltpu.VMEM((n_y, n_a, piece, 4 * chans), F32),
                 pltpu.VMEM((n_y, piece, 4 * chans), F32),
                 pltpu.VMEM((n_y, piece, 4 * chans), F32),
                 pltpu.VMEM((n_z, piece, 4 * chans), F32),
                 pltpu.VMEM((n_a, n_y, piece, 4 * chans), F32),
                 dma((8,)), dma((8,)),
-                dma((n_a,)), dma((n_a,)),
-                dma((n_y,)), dma((n_y,)),
-                dma((n_z,)), dma((n_z,)),
-                dma((n_y,)), dma((n_y,)),
-                dma((n_a,)), dma((n_a,)),
+                dma, dma((n_y,)),
+                dma, dma,
+                dma, dma,
+                dma, dma((n_y,)),
+                dma, dma,
             ],
             compiler_params=pltpu.CompilerParams(collective_id=0, has_side_effects=True),
         )(

time: 48.3 us -> 43.5 us (0.901)
  Pallas kernels: 44.1 us -> 41.3 us
  local copies, waits for them, and re-layouts: 3.41 us -> 1.42 us
    pallas_call x1, Pallas kernels: 44.1 us -> 41.3 us  [step(): pl.pallas_call(functools.partial(kernel, sizes, 1.0 / math.sqrt(cells)),...]
    unnamed x2, local copies, waits for them, and re-layouts: 3.41 us -> 1.42 us
where the time goes in v2:
time: 43.5 us; the launch traced here: 43.4 us
  Pallas kernels  41.3 us (95%)
  local copies, waits for them, and re-layouts  1.42 us (3%)
  between operations  0.64 us (1%)
    pallas_call x1, Pallas kernels, step(): pl.pallas_call(functools.partial(kernel, sizes, 1.0 / math.sqrt(cells)),...  41.3 us
    unnamed x2, local copies, waits for them, and re-layouts  1.42 us

profile of v2, /device:TPU:1, one launch (start us, length us, event | category | flops | bytes accessed | tf_op | source)
XLA Modules:
  0.0 43.4 jit_solution(14838151004985830752)
XLA Ops:
  0.6 41.3 %shard_map.50 = (bf16[512,128]{1,0:T(8,128)(2,1)S(1)}, f32[864,32]{1,0:T(8,128)S(1)}) custom-call(bf16[512,128]{1,0:T(8,128)(2,1)} %bitcast.8, bf16[512,128]{1,0:T(8,128)(2,1)} %bitcast.9, bf16[864,32]{1,0:T(8,128)(2,1)} %bitcast.7), custom_call_target="tpu_custom_call" | custom-call | tf_op jit(solution)/shard_map/pallas_call | solution.py:267
  41.9 0.7 %copy.7 = bf16[32,4,4,128]{3,2,1,0:T(4,128)(2,1)} copy(bf16[32,4,4,128]{3,2,1,0:T(4,128)(2,1)S(1)} %bitcast.6) | data formatting | bytes 262144
  42.6 0.8 %copy.8 = f32[3,3,3,32,32]{4,3,2,1,0:T(8,128)} copy(f32[3,3,3,32,32]{4,3,2,1,0:T(8,128)S(1)} %bitcast.5) | data formatting | bytes 221184
